TPU v7x, 256 devices: a whole 4x4x8 slice. The times are simulated.
256 devices in a mesh: gx: 4 (over y), gy: 8 (over x, core), gz: 8 (over z).
Axes of the slice: x: 4, y: 4, z: 8, core: 2. Of those that a mesh axis runs over, the one named last changes fastest.
Arguments:
- positions: float32 [3, 4, 8, 8, 128], P(None, 'gx', 'gy', 'gz'), may hold values from 0 to 22
- elements: int32 [4, 8, 8, 128], P('gx', 'gy', 'gz'), may hold values from 0 to 3
- prior_charges: float32 [4, 8, 8, 128], P('gx', 'gy', 'gz'), may hold values from -1.8 to 1.8
- neighbours: int32 [4, 8, 8, 128, 128], P('gx', 'gy', 'gz'), may hold values from 0 to 959, all different within a row; in each aligned block of 128 rows (0 to 127, 128 to 255, ..., all dimensions but the last counted through in order) at most 19 rows name the same one
- counts: int32 [4, 8, 8, 128], P('gx', 'gy', 'gz'), may hold values from 64 to 128
- boundary: int32 [4, 8, 8, 32], P('gx', 'gy', 'gz'), may hold values from 0 to 127, as said below
- wave_numbers: int32 [3, 2048], replicated, may hold values from -6 to 6, as said below
- hardness: float32 [4], replicated, may hold values from 3 to 9
- chi_first: bfloat16 [4, 32, 128], replicated, may hold values from -0.5 to 0.5
- chi_bias: float32 [4, 32], replicated, may hold values from -3 to 3
- chi_mid: bfloat16 [32, 4, 32], replicated, may hold values from -1 to 1
- chi_out: float32 [4, 32], replicated, may hold values from -1 to 1
- chi_offset: float32 [4], replicated, may hold values from -3 to 3
- short_first: bfloat16 [4, 32, 256], replicated, may hold values from -0.375 to 0.375
- short_charge: float32 [4, 32], replicated, may hold values from -4 to 4
- short_bias: float32 [4, 32], replicated, may hold values from -3 to 3
- short_mid: bfloat16 [32, 4, 32], replicated, may hold values from -1 to 1
- short_out: float32 [4, 32], replicated, may hold values from -1 to 1
- short_offset: float32 [4], replicated, may hold values from -3 to 3
Outputs:
- charges: float32 [4, 8, 8, 128], P('gx', 'gy', 'gz')
- energies: float32 [4, 8, 8, 128], P('gx', 'gy', 'gz')
Inputs may be any that keep to these rules, and one draw needn't show every extreme that they name: `neighbours`: each row names 128 different indices; within one domain no index is named by more than 19 rows, a bound that some block reaches. `boundary`: the 32 indices of a domain are different. `wave_numbers`: every entry is nonzero.
All inputs are finite; a program needn't handle non-finite values.
Results may differ from a plain program's by a relative error of at most 0.0014.
Values sent between devices are 32-bit elements; how exact they have to be, the bound alone decides.
A program may use at most 64 MiB of HBM per device.

v0:
```python
import functools

import jax
import jax.numpy as jnp
import numpy as np
from jax import lax
from jax.sharding import Mesh
from jax.sharding import PartitionSpec as P

NBASIS = 32
ITERS = 3
GX_GY_GZ = ("gx", "gy_0", "gy_1", "gz")
GY = ("gy_0", "gy_1")


DOMAIN = 22.0
SOFTENING = 22.0
SCREENING = 0.005
CUTOFF = 66.0
DAMPING = 0.1
COUPLING = 64.0
FEATURE_SCALE = 0.5
PAIR_STRENGTH = 1.0


def with_halo(x, sides, width):
    for axis, dim in sides:
        size, length = (lax.axis_size(axis), x.shape[dim])
        up = [(i, (i + 1) % size) for i in range(size)]
        down = [(j, i) for i, j in up]
        last = lax.slice_in_dim(x, length - width, length, axis=dim)
        initial = lax.slice_in_dim(x, 0, width, axis=dim)
        before = lax.ppermute(last, axis, up)
        after = lax.ppermute(initial, axis, down)
        x = jnp.concatenate([before, x, after], axis=dim)
    return x


def over_axes(x, axes):
    return functools.reduce(lax.psum, axes, x)


def neighbour_offsets():
    table = []
    for first in range(3):
        for second in range(3):
            for third in range(3):
                if first * 9 + second * 3 + third != 13:
                    table.append((first - 1, second - 1, third - 1))
    return table


def pair_terms(own_place, gathered, slot_counts):
    slots = gathered.shape[2]
    separation = gathered[:3] - own_place[:, :, None]
    distance = jnp.sqrt(jnp.sum(separation * separation, axis=0))
    valid = (jnp.arange(slots, dtype=jnp.int32)[None, :] < slot_counts[:, None]).astype(jnp.float32)
    soft = jnp.sqrt(distance * distance + SOFTENING * SOFTENING)
    kernel = valid * (PAIR_STRENGTH / slots) * SOFTENING * lax.erfc(SCREENING * soft) / soft
    spacing = CUTOFF / (NBASIS - 1)
    centres = spacing * jnp.arange(NBASIS, dtype=jnp.float32)
    taper = valid * 0.5 * (1.0 + jnp.cos(jnp.pi * jnp.minimum(distance, CUTOFF) / CUTOFF))
    basis = jnp.exp(-0.5 * ((distance[None] - centres[:, None, None]) / spacing) ** 2) * taper[None]
    return (kernel, basis)


def contract_slots(basis, weights):
    blocks = [jnp.sum(basis * weights[kind][None], axis=2) for kind in range(weights.shape[0])]
    return jnp.concatenate(blocks, axis=0)


def element_network(features, kinds, weight_first, bias, weight_mid, weight_out, offset, extra):
    count, hidden, width = weight_first.shape
    activation = jnp.dot(
        weight_first.reshape(count * hidden, width), features, preferred_element_type=jnp.float32
    )
    activation = activation + bias.reshape(count * hidden, 1) + extra
    mask = jnp.repeat(kinds, hidden, axis=0)
    first = (jnp.tanh(activation) * mask).astype(jnp.bfloat16)
    second = jnp.tanh(
        jnp.dot(
            weight_mid.reshape(hidden, count * hidden), first, preferred_element_type=jnp.float32
        )
    )
    chosen = jnp.sum(weight_out[:, :, None] * kinds[:, None, :], axis=0)
    return jnp.sum(second * chosen, axis=0) + jnp.sum(offset[:, None] * kinds, axis=0)


def phase_tile(waves, placed):
    theta = (
        waves[0][:, None] * placed[0][None, :]
        + waves[1][:, None] * placed[1][None, :]
        + waves[2][:, None] * placed[2][None, :]
    )
    return jnp.concatenate([jnp.cos(theta), jnp.sin(theta)], axis=0)


def drop_centre(blocks):
    return jnp.concatenate([blocks[..., :13, :], blocks[..., 14:, :]], axis=-2)


def body(
    positions,
    elements,
    prior_charges,
    neighbours,
    counts,
    boundary,
    wave_numbers,
    hardness,
    chi_first,
    chi_bias,
    chi_mid,
    chi_out,
    chi_offset,
    short_first,
    short_charge,
    short_bias,
    short_mid,
    short_out,
    short_offset,
):
    atoms = positions.shape[-1]
    kinds_count = hardness.shape[0]
    own_place = positions.reshape(3, atoms)
    kinds = (
        elements.reshape(1, atoms) == jnp.arange(kinds_count, dtype=jnp.int32)[:, None]
    ).astype(jnp.float32)
    neighbour_list = neighbours.reshape(atoms, -1)
    slot_counts = counts.reshape(atoms)
    picks = boundary.reshape(-1)
    rows = jnp.concatenate([own_place, kinds, prior_charges.reshape(1, atoms)], axis=0)
    width = rows.shape[0]
    sent = rows[:, picks].reshape(width, 1, 1, 1, -1)
    near = with_halo(sent, (("gx", 1), (GY, 2), ("gz", 3)), 1)
    ghost_rows = drop_centre(near.reshape(width, 27, -1))
    shifts = DOMAIN * np.array(neighbour_offsets(), dtype=np.float32).T
    ghost_rows = jnp.concatenate(
        [ghost_rows[:3] + shifts[:, :, None], ghost_rows[3:]], axis=0
    ).reshape(width, -1)
    extended = jnp.concatenate([rows, ghost_rows], axis=1)
    gathered = extended[:, neighbour_list]
    kernel, basis = pair_terms(own_place, gathered, slot_counts)
    kinds_near = gathered[3 : 3 + kinds_count]
    descriptor = contract_slots(basis, kinds_near)
    features = (FEATURE_SCALE * descriptor).astype(jnp.bfloat16)
    negativity = element_network(
        features, kinds, chi_first, chi_bias, chi_mid, chi_out, chi_offset, 0.0
    )
    stiffness = jnp.sum(hardness[:, None] * kinds, axis=0)
    axis_sizes = (lax.axis_size("gx"), lax.axis_size(GY), lax.axis_size("gz"))
    anchor = DOMAIN * jnp.stack(
        [lax.axis_index("gx"), lax.axis_index(GY), lax.axis_index("gz")]
    ).astype(jnp.float32)
    placed = own_place + anchor[:, None]
    box = DOMAIN * np.array(axis_sizes, dtype=np.float32)
    waves = 2.0 * np.pi * wave_numbers.astype(jnp.float32) / box[:, None]
    squared = jnp.sum(waves * waves, axis=0)
    total_atoms = atoms * axis_sizes[0] * axis_sizes[1] * axis_sizes[2]
    wave_weights = (
        COUPLING * DAMPING**2 * jnp.exp(-squared / (4.0 * DAMPING**2)) / (squared * total_atoms)
    )
    wave_weights = jnp.concatenate([wave_weights, wave_weights])
    tile = phase_tile(waves, placed)

    def structure(vector):
        return jnp.sum(tile * vector[None, :], axis=1)

    def spread(weighted):
        return jnp.sum(weighted[:, None] * tile, axis=0)

    def local_apply(vector, ghost):
        values = jnp.concatenate([vector, ghost])
        return stiffness * vector + jnp.sum(kernel * values[neighbour_list], axis=1)

    def charge_halo(vector):
        sent_values = vector[picks].reshape(1, 1, 1, -1)
        received = with_halo(sent_values, (("gx", 0), (GY, 1), ("gz", 2)), 1)
        return drop_centre(received.reshape(27, -1)).reshape(-1)

    def reduce_structure(partial_value, extras):
        total, sums = (over_axes(partial_value, GX_GY_GZ), over_axes(extras, GX_GY_GZ))
        weighted = wave_weights * total
        return (weighted, sums, jnp.sum(weighted * total))

    charges = prior_charges.reshape(atoms)
    ghost_charge = ghost_rows[-1]
    start_local = local_apply(charges, ghost_charge)
    start_weighted = reduce_structure(structure(charges), jnp.zeros((0,), jnp.float32))[0]
    residual = -negativity - (start_local + spread(start_weighted))
    ghost_residual = charge_halo(residual)
    local = local_apply(residual, ghost_residual)
    weighted, sums, energy = reduce_structure(
        structure(residual), jnp.stack([jnp.sum(residual * residual), jnp.sum(residual * local)])
    )
    norm_now = sums[0]
    curvature = sums[1] + energy
    image = local + spread(weighted)
    direction = residual
    local_direction = local
    ghost_direction = ghost_residual
    alpha = norm_now / curvature
    for step in range(ITERS):
        charges = charges + alpha * direction
        ghost_charge = ghost_charge + alpha * ghost_direction
        if step + 1 < ITERS:
            residual = residual - alpha * image
            ghost_residual = charge_halo(residual)
            local = local_apply(residual, ghost_residual)
            weighted, sums, energy = reduce_structure(
                structure(residual),
                jnp.stack(
                    [
                        jnp.sum(residual * residual),
                        jnp.sum(residual * local),
                        jnp.sum(residual * image),
                        jnp.sum(direction * local),
                        jnp.sum(residual * local_direction),
                    ]
                ),
            )
            ratio = sums[0] / norm_now
            image = local + spread(weighted) + ratio * image
            local_direction = local + ratio * local_direction
            cross = 2.0 * sums[2] + sums[3] - sums[4]
            curvature = sums[1] + energy + ratio * cross + ratio * ratio * curvature
            direction = residual + ratio * direction
            ghost_direction = ghost_residual + ratio * ghost_direction
            alpha = sums[0] / curvature
            norm_now = sums[0]
    extended_charge = jnp.concatenate([charges, ghost_charge])
    weighted_kinds = kinds_near * extended_charge[neighbour_list][None]
    charge_descriptor = contract_slots(basis, weighted_kinds)
    inputs_short = (
        FEATURE_SCALE * jnp.concatenate([descriptor, charge_descriptor], axis=0)
    ).astype(jnp.bfloat16)
    energies = element_network(
        inputs_short,
        kinds,
        short_first,
        short_bias,
        short_mid,
        short_out,
        short_offset,
        short_charge.reshape(-1, 1) * charges[None, :],
    )
    return (charges.reshape(1, 1, 1, atoms), energies.reshape(1, 1, 1, atoms))


def solution(mesh):
    split = Mesh(
        mesh.devices.reshape(mesh.shape["gx"], 4, 2, mesh.shape["gz"]), ("gx", "gy_0", "gy_1", "gz")
    )
    return jax.shard_map(
        body,
        mesh=split,
        in_specs=(
            P(None, "gx", GY, "gz", None),
            P("gx", GY, "gz", None),
            P("gx", GY, "gz", None),
            P("gx", GY, "gz", None, None),
            P("gx", GY, "gz", None),
            P("gx", GY, "gz", None),
            P(),
            P(),
            P(),
            P(),
            P(),
            P(),
            P(),
            P(),
            P(),
            P(),
            P(),
            P(),
            P(),
        ),
        out_specs=(P("gx", GY, "gz", None), P("gx", GY, "gz", None)),
        check_vma=False,
    )
```

profile of v0, /device:TPU:1, one launch (start us, length us, event | category | flops | bytes accessed | tf_op | source)
XLA Modules:
  0.0 757.6 jit_solution(13459137677029703835)
XLA Ops:
  14.9 12.0 %psum.196 = f32[4096]{0:T(1024)S(1)} all-reduce(f32[4096]{0:T(1024)S(1)} %multiply_reduce_fusion.10), channel_id=1, replica_groups=mesh['gx'=4,'gy_0'=4,'gy_1'=2,'gz'=8] {'gx'}, use_global_device_ids=true, to_apply=%region_12.0 | all-reduce | flops 4096 | bytes 32768 | tf_op jit(solution)/shard_map/psum | solution.py:40
  27.0 13.1 %psum.197 = f32[4096]{0:T(1024)S(1)} all-reduce(f32[4096]{0:T(1024)S(1)} %psum.196), channel_id=1, replica_groups=mesh['gx'=4,'gy_0'=4,'gy_1'=2,'gz'=8] {'gy_0'}, use_global_device_ids=true, to_apply=%region_13.0 | all-reduce | flops 4096 | bytes 32768 | tf_op jit(solution)/shard_map/psum | solution.py:40
  40.1 11.9 %psum.198 = f32[4096]{0:T(1024)S(1)} all-reduce(f32[4096]{0:T(1024)S(1)} %psum.197), channel_id=1, replica_groups=mesh['gx'=4,'gy_0'=4,'gy_1'=2,'gz'=8] {'gy_1'}, use_global_device_ids=true, to_apply=%region_14.0 | all-reduce | flops 4096 | bytes 32768 | tf_op jit(solution)/shard_map/psum | solution.py:40
  52.0 25.8 %psum.199 = f32[4096]{0:T(1024)S(1)} all-reduce(f32[4096]{0:T(1024)S(1)} %psum.198), channel_id=1, replica_groups=mesh['gx'=4,'gy_0'=4,'gy_1'=2,'gz'=8] {'gz'}, use_global_device_ids=true, to_apply=%region_15.0 | all-reduce | flops 4096 | bytes 32768 | tf_op jit(solution)/shard_map/psum | solution.py:40
  94.2 54.4 %gather_fusion.1 = f32[16384,8]{1,0:T(8,128)} fusion(f32[8,960]{0,1:T(8,128)S(1)} %copy.59, s32[16384]{0:T(1024)S(1)} %fusion.28), kind=kCustom, calls=%fused_computation.1 | custom fusion | bytes 1114112 | tf_op jit(solution)/shard_map/gather | solution.py:142
  154.1 65.3 %gather_fusion.2 = f32[16384]{0:T(1024)S(1)} fusion(f32[960]{0:T(1024)S(1)} %pad_maximum_fusion.18, s32[16384]{0:T(1024)S(1)} %fusion.28), kind=kCustom, calls=%fused_computation.2 | custom fusion | bytes 196608 | tf_op jit(solution)/shard_map/gather | solution.py:174
  240.0 65.3 %gather_fusion.4 = f32[16384]{0:T(1024)S(1)} fusion(f32[960]{0:T(1024)S(1)} %pad_maximum_fusion.19, s32[16384]{0:T(1024)S(1)} %fusion.28), kind=kCustom, calls=%fused_computation.4 | custom fusion | bytes 196608 | tf_op jit(solution)/shard_map/gather | solution.py:174
  307.4 14.0 %all-reduce.8 = (f32[4096]{0:T(1024)S(1)}, f32[2]{0:T(128)S(1)}) all-reduce(f32[4096]{0:T(1024)S(1)} %multiply_reduce_fusion.8, f32[2]{0:T(128)S(1)} %pad_maximum_fusion.26), channel_id=1, replica_groups=mesh['gx'=4,'gy_0'=4,'gy_1'=2,'gz'=8] {'gx'}, use_global_device_ids=true, to_apply=%region_25.0 | all-reduce | flops 4098 | bytes 32784 | tf_op jit(solution)/shard_map/psum | solution.py:40
  321.4 16.3 %all-reduce.5 = (f32[4096]{0:T(1024)S(1)}, f32[2]{0:T(128)S(1)}) all-reduce(f32[4096]{0:T(1024)S(1)} %get-tuple-element.45, f32[2]{0:T(128)S(1)} %get-tuple-element.46), channel_id=1, replica_groups=mesh['gx'=4,'gy_0'=4,'gy_1'=2,'gz'=8] {'gy_0'}, use_global_device_ids=true, to_apply=%region_26.0 | all-reduce | flops 4098 | bytes 32784 | tf_op jit(solution)/shard_map/psum | solution.py:40
  337.7 9.1 %all-reduce.11 = (f32[4096]{0:T(1024)S(1)}, f32[2]{0:T(128)S(1)}) all-reduce(f32[4096]{0:T(1024)S(1)} %get-tuple-element.39, f32[2]{0:T(128)S(1)} %get-tuple-element.40), channel_id=1, replica_groups=mesh['gx'=4,'gy_0'=4,'gy_1'=2,'gz'=8] {'gy_1'}, use_global_device_ids=true, to_apply=%region_27.0 | all-reduce | flops 4098 | bytes 32784 | tf_op jit(solution)/shard_map/psum | solution.py:40
  346.8 23.0 %all-reduce.2 = (f32[4096]{0:T(1024)S(1)}, f32[2]{0:T(128)S(1)}) all-reduce(f32[4096]{0:T(1024)S(1)} %get-tuple-element.51, f32[2]{0:T(128)S(1)} %get-tuple-element.52), channel_id=1, replica_groups=mesh['gx'=4,'gy_0'=4,'gy_1'=2,'gz'=8] {'gz'}, use_global_device_ids=true, to_apply=%region_28.0 | all-reduce | flops 4098 | bytes 32784 | tf_op jit(solution)/shard_map/psum | solution.py:40
  378.9 8.6 %collective-permute-start.14 = (f32[3,1,1,32]{3,2,1,0:T(1,128)S(1)}, f32[3,1,1,32]{3,2,1,0:T(1,128)S(1)}, u32[]{:S(2)}, u32[]{:S(2)}) collective-permute-start(f32[3,1,1,32]{3,2,1,0:T(1,128)S(1)} %pad_maximum_fusion.24), channel_id=1, source_target_pairs={{0,8},{8,16},{16,24},{24,32},{32,40},{40,48},{48,56},{56,0},{1,9},... | collective-permute-start | bytes 1160 | tf_op jit(solution)/shard_map/ppermute | solution.py:33
  394.7 65.3 %gather_fusion.6 = f32[16384]{0:T(1024)S(1)} fusion(f32[960]{0:T(1024)S(1)} %pad_maximum_fusion.20, s32[16384]{0:T(1024)S(1)} %fusion.28), kind=kCustom, calls=%fused_computation.6 | custom fusion | bytes 196608 | tf_op jit(solution)/shard_map/gather | solution.py:174
  463.8 13.8 %all-reduce.7 = (f32[4096]{0:T(1024)S(1)}, f32[5]{0:T(128)S(1)}) all-reduce(f32[4096]{0:T(1024)S(1)} %multiply_reduce_fusion.6, f32[5]{0:T(128)S(1)} %stack.69), channel_id=1, replica_groups=mesh['gx'=4,'gy_0'=4,'gy_1'=2,'gz'=8] {'gx'}, use_global_device_ids=true, to_apply=%region_42.0 | all-reduce | flops 4101 | bytes 32808 | tf_op jit(solution)/shard_map/psum | solution.py:40
  477.7 13.8 %all-reduce.4 = (f32[4096]{0:T(1024)S(1)}, f32[5]{0:T(128)S(1)}) all-reduce(f32[4096]{0:T(1024)S(1)} %get-tuple-element.43, f32[5]{0:T(128)S(1)} %get-tuple-element.44), channel_id=1, replica_groups=mesh['gx'=4,'gy_0'=4,'gy_1'=2,'gz'=8] {'gy_0'}, use_global_device_ids=true, to_apply=%region_43.0 | all-reduce | flops 4101 | bytes 32808 | tf_op jit(solution)/shard_map/psum | solution.py:40
  491.5 9.7 %all-reduce.10 = (f32[4096]{0:T(1024)S(1)}, f32[5]{0:T(128)S(1)}) all-reduce(f32[4096]{0:T(1024)S(1)} %get-tuple-element.37, f32[5]{0:T(128)S(1)} %get-tuple-element.38), channel_id=1, replica_groups=mesh['gx'=4,'gy_0'=4,'gy_1'=2,'gz'=8] {'gy_1'}, use_global_device_ids=true, to_apply=%region_44.0 | all-reduce | flops 4101 | bytes 32808 | tf_op jit(solution)/shard_map/psum | solution.py:40
  501.2 23.1 %all-reduce.1 = (f32[4096]{0:T(1024)S(1)}, f32[5]{0:T(128)S(1)}) all-reduce(f32[4096]{0:T(1024)S(1)} %get-tuple-element.49, f32[5]{0:T(128)S(1)} %get-tuple-element.50), channel_id=1, replica_groups=mesh['gx'=4,'gy_0'=4,'gy_1'=2,'gz'=8] {'gz'}, use_global_device_ids=true, to_apply=%region_45.0 | all-reduce | flops 4101 | bytes 32808 | tf_op jit(solution)/shard_map/psum | solution.py:40
  536.4 8.2 %collective-permute-start.20 = (f32[3,1,1,32]{3,2,1,0:T(1,128)S(1)}, f32[3,1,1,32]{3,2,1,0:T(1,128)S(1)}, u32[]{:S(2)}, u32[]{:S(2)}) collective-permute-start(f32[3,1,1,32]{3,2,1,0:T(1,128)S(1)} %pad_maximum_fusion.25), channel_id=1, source_target_pairs={{0,8},{8,16},{16,24},{24,32},{32,40},{40,48},{48,56},{56,0},{1,9},... | collective-permute-start | bytes 1160 | tf_op jit(solution)/shard_map/ppermute | solution.py:33
  551.5 65.3 %gather_fusion.8 = f32[16384]{0:T(1024)S(1)} fusion(f32[960]{0:T(1024)S(1)} %pad_maximum_fusion.21, s32[16384]{0:T(1024)S(1)} %fusion.28), kind=kCustom, calls=%fused_computation.8 | custom fusion | bytes 196608 | tf_op jit(solution)/shard_map/gather | solution.py:174
  620.8 13.7 %all-reduce.6 = (f32[5]{0:T(128)S(1)}, f32[4096]{0:T(1024)S(1)}) all-reduce(f32[5]{0:T(128)S(1)} %stack.75, f32[4096]{0:T(1024)S(1)} %multiply_reduce_fusion.4), channel_id=1, replica_groups=mesh['gx'=4,'gy_0'=4,'gy_1'=2,'gz'=8] {'gx'}, use_global_device_ids=true, to_apply=%region_54.0 | all-reduce | flops 4101 | bytes 32808 | tf_op jit(solution)/shard_map/psum | solution.py:40
  634.5 14.9 %all-reduce.3 = (f32[5]{0:T(128)S(1)}, f32[4096]{0:T(1024)S(1)}) all-reduce(f32[5]{0:T(128)S(1)} %get-tuple-element.41, f32[4096]{0:T(1024)S(1)} %get-tuple-element.42), channel_id=1, replica_groups=mesh['gx'=4,'gy_0'=4,'gy_1'=2,'gz'=8] {'gy_0'}, use_global_device_ids=true, to_apply=%region_55.0 | all-reduce | flops 4101 | bytes 32808 | tf_op jit(solution)/shard_map/psum | solution.py:40
  649.4 9.2 %all-reduce.9 = (f32[5]{0:T(128)S(1)}, f32[4096]{0:T(1024)S(1)}) all-reduce(f32[5]{0:T(128)S(1)} %get-tuple-element.35, f32[4096]{0:T(1024)S(1)} %get-tuple-element.36), channel_id=1, replica_groups=mesh['gx'=4,'gy_0'=4,'gy_1'=2,'gz'=8] {'gy_1'}, use_global_device_ids=true, to_apply=%region_56.0 | all-reduce | flops 4101 | bytes 32808 | tf_op jit(solution)/shard_map/psum | solution.py:40
  658.5 23.1 %all-reduce = (f32[5]{0:T(128)S(1)}, f32[4096]{0:T(1024)S(1)}) all-reduce(f32[5]{0:T(128)S(1)} %get-tuple-element.47, f32[4096]{0:T(1024)S(1)} %get-tuple-element.48), channel_id=1, replica_groups=mesh['gx'=4,'gy_0'=4,'gy_1'=2,'gz'=8] {'gz'}, use_global_device_ids=true, to_apply=%region_57.0 | all-reduce | flops 4101 | bytes 32808 | tf_op jit(solution)/shard_map/psum | solution.py:40
  688.6 65.3 %gather_fusion.9 = f32[16384]{0:T(1024)S(1)} fusion(f32[960]{0:T(1024)S(1)} %pad_maximum_fusion.22, s32[16384]{0:T(1024)S(1)} %fusion.28), kind=kCustom, calls=%fused_computation.9 | custom fusion | bytes 196608 | tf_op jit(solution)/shard_map/gather | solution.py:232
  (215 shorter events, 100.3 us)
Async XLA Ops:
  4.1 76.3 %collective-permute-start = (f32[8,1,1,1,32]{0,4,3,2,1:T(8,128)S(1)}, f32[8,1,1,1,32]{0,4,3,2,1:T(8,128)S(1)}, u32[]{:S(2)}, u32[]{:S(2)}) collective-permute-start(f32[8,1,1,1,32]{0,4,3,2,1:T(8,128)S(1)} %bitcast.224), channel_id=1, source_target_pairs={{0,64},{64,128},{128,192},{192,0},{1,65},{65,129},{129,193},{193,1... | collective-permute-start | bytes 3080 | tf_op jit(solution)/shard_map/ppermute | solution.py:33
  6.2 74.2 %collective-permute-start.1 = (f32[8,1,1,1,32]{0,4,3,2,1:T(8,128)S(1)}, f32[8,1,1,1,32]{0,4,3,2,1:T(8,128)S(1)}, u32[]{:S(2)}, u32[]{:S(2)}) collective-permute-start(f32[8,1,1,1,32]{0,4,3,2,1:T(8,128)S(1)} %bitcast.225), channel_id=1, source_target_pairs={{64,0},{128,64},{192,128},{0,192},{65,1},{129,65},{193,129},{1,193... | collective-permute-start | bytes 3080 | tf_op jit(solution)/shard_map/ppermute | solution.py:34
  80.5 7.9 %collective-permute-start.2 = (f32[8,3,1,1,32]{4,0,3,2,1:T(8,128)S(1)}, f32[8,3,1,1,32]{4,0,3,2,1:T(8,128)S(1)}, u32[]{:S(2)}, u32[]{:S(2)}) collective-permute-start(f32[8,3,1,1,32]{4,0,3,2,1:T(8,128)S(1)} %pad_maximum_fusion.13), channel_id=1, source_target_pairs={{0,8},{8,16},{16,24},{24,32},{32,40},{40,48},{48,56},{56,0},{1,9},... | collective-permute-start | bytes 9224 | tf_op jit(solution)/shard_map/ppermute | solution.py:33
  85.9 3.1 collective-permute-start.3
  89.0 4.7 collective-permute-start.4
  89.0 4.7 collective-permute-start.5
  226.4 3.7 collective-permute-start.6
  226.5 3.6 collective-permute-start.7
  230.1 5.8 collective-permute-start.8
  231.9 4.0 collective-permute-start.9
  235.9 3.9 collective-permute-start.10
  236.0 3.8 collective-permute-start.11
  375.2 3.7 collective-permute-start.12
  375.3 3.6 collective-permute-start.13
  378.9 9.3 %collective-permute-start.14 = (f32[3,1,1,32]{3,2,1,0:T(1,128)S(1)}, f32[3,1,1,32]{3,2,1,0:T(1,128)S(1)}, u32[]{:S(2)}, u32[]{:S(2)}) collective-permute-start(f32[3,1,1,32]{3,2,1,0:T(1,128)S(1)} %pad_maximum_fusion.24), channel_id=1, source_target_pairs={{0,8},{8,16},{16,24},{24,32},{32,40},{40,48},{48,56},{56,0},{1,9},... | collective-permute-start | bytes 1160 | tf_op jit(solution)/shard_map/ppermute | solution.py:33
  387.5 3.3 collective-permute-start.15
  390.8 3.7 collective-permute-start.16
  390.9 3.7 collective-permute-start.17
  532.7 3.7 collective-permute-start.18
  532.8 3.6 collective-permute-start.19
  536.4 9.0 %collective-permute-start.20 = (f32[3,1,1,32]{3,2,1,0:T(1,128)S(1)}, f32[3,1,1,32]{3,2,1,0:T(1,128)S(1)}, u32[]{:S(2)}, u32[]{:S(2)}) collective-permute-start(f32[3,1,1,32]{3,2,1,0:T(1,128)S(1)} %pad_maximum_fusion.25), channel_id=1, source_target_pairs={{0,8},{8,16},{16,24},{24,32},{32,40},{40,48},{48,56},{56,0},{1,9},... | collective-permute-start | bytes 1160 | tf_op jit(solution)/shard_map/ppermute | solution.py:33
  544.5 3.0 collective-permute-start.21
  547.6 3.7 collective-permute-start.22
  547.6 3.7 collective-permute-start.23
  (25 other events, 2371.5 us)
where the time goes:
time: 763 us; the launch traced here: 758 us
  local copies, waits for them, and re-layouts  401 us (53%)
  blocking collectives  247 us (32%)
  starting transfers between devices  52.1 us (7%)
  other arithmetic  32.2 us (4%)
  between operations  13.3 us (2%)
  waiting for transfers between devices  10.5 us (1%)
    gather x4, local copies, waits for them, and re-layouts, local_apply(): return stiffness * vector + jnp.sum(kernel * values[neighbour_list], axis=1)  261 us
    psum x16, blocking collectives, over_axes(): return functools.reduce(lax.psum, axes, x)  247 us
    gather x1, local copies, waits for them, and re-layouts, body(): weighted_kinds = kinds_near * extended_charge[neighbour_list][None]  65.3 us
    gather x2, local copies, waits for them, and re-layouts, body(): gathered = extended[:, neighbour_list]  59.6 us
    ppermute x12, starting transfers between devices, with_halo(): before = lax.ppermute(last, axis, up)  26.5 us
    ppermute x12, starting transfers between devices, with_halo(): after = lax.ppermute(initial, axis, down)  25.6 us
  transfers between devices with their start and end apart: 24, of which 11 were waited for; matrix products, arithmetic and copies ran while one was open for 2% of the time, Pallas kernels for 0%

commit v1 on v0

v1 whole, which is shorter than its diff:
```python
import functools
import math

import jax
import jax.numpy as jnp
from jax import lax
from jax.experimental import pallas as pl
from jax.experimental.pallas import tpu as pltpu
from jax.sharding import PartitionSpec as P

ATOMS = 128
ELEM = 4
HID = 32
NBASIS = 32
ITERS = 3
AXES = ("gx", "gy", "gz")

DOMAIN = 22.0
SOFTENING = 22.0
SCREENING = 0.005
CUTOFF = 66.0
DAMPING = 0.1
COUPLING = 64.0
FEATURE_SCALE = 0.5
PAIR_STRENGTH = 1.0

STAGES = ("gy", "gx", "gz")
OFFSETS = [(a, b, c) for a in (-1, 0, 1) for b in (-1, 0, 1) for c in (-1, 0, 1) if (a, b, c) != (0, 0, 0)]
BLOCKS = len(OFFSETS)
WAVE_LANES = 96

F32 = jnp.float32
BF16 = jnp.bfloat16
HIGHEST = lax.Precision.HIGHEST


def iota(shape, dim):
    return lax.broadcasted_iota(jnp.int32, shape, dim)


def take_lanes(table, lanes):
    return jnp.take_along_axis(table, lanes, axis=1, mode="promise_in_bounds")


def dot(a, b, precision=None):
    return lax.dot_general(a, b, (((1,), (0,)), ((), ())), precision=precision, preferred_element_type=F32)


def total(x):
    return jnp.sum(jnp.sum(x, axis=0, keepdims=True), axis=1, keepdims=True)


def kernel(
    sizes,
    positions, elements, prior, neighbours, counts, boundary, waves,
    hardness, chi_first, chi_bias, chi_mid, chi_out, chi_offset,
    short_first, short_charge, short_bias, short_mid, short_out, short_offset,
    charges_out, energies_out,
    own_rows, places_in, places_got, row_out, row_got, part_out, gy_got, gx_got, gz_got,
    lanes, chunks, seen, pair, falloff, spans, tables, harmonics, phases, phases_t, coarse, ledger,
    halo_send, halo_recv, sum_send, sum_recv,
):
    at = {name: lax.axis_index(name) for name in AXES}

    def stepped(name, shift):
        return lax.rem(at[name] + (shift + sizes[name]), sizes[name])

    def device(shift):
        return tuple(stepped(name, s) if s else at[name] for name, s in zip(AXES, shift))

    partners = set(OFFSETS)
    for place, name in enumerate(AXES):
        for step in range(1, sizes[name]):
            step = step if step <= sizes[name] // 2 else step - sizes[name]
            partners.add(tuple(step if place == axis else 0 for axis in range(3)))
    barrier = pltpu.get_barrier_semaphore()
    for shift in sorted(partners):
        pl.semaphore_signal(barrier, inc=1, device_id=device(shift), device_id_type=pl.DeviceIdType.MESH)

    def send_blocks(source, slots, index):
        for number, shift in enumerate(OFFSETS):
            pltpu.make_async_remote_copy(
                src_ref=source, dst_ref=slots.at[number],
                send_sem=halo_send.at[index], recv_sem=halo_recv.at[index],
                device_id=device(tuple(-s for s in shift)), device_id_type=pl.DeviceIdType.MESH,
            ).start()

    def wait_blocks(slots, sems, index):
        pltpu.make_async_copy(slots, slots, sems.at[index]).wait()

    got = {"gy": gy_got, "gx": gx_got, "gz": gz_got}

    def send_part(number, stage, value):
        name = STAGES[stage]
        part_out[number, stage] = value
        for step in range(1, sizes[name]):
            pltpu.make_async_remote_copy(
                src_ref=part_out.at[number, stage], dst_ref=got[name].at[number, step - 1],
                send_sem=sum_send.at[number, stage], recv_sem=sum_recv.at[number, stage],
                device_id=device(tuple(step if axis == name else 0 for axis in AXES)),
                device_id_type=pl.DeviceIdType.MESH,
            ).start()

    def summed(number, stage, value):
        slots = got[STAGES[stage]].at[number]
        pltpu.make_async_copy(slots, slots, sum_recv.at[number, stage]).wait()
        for step in range(1, sizes[STAGES[stage]]):
            value = value + got[STAGES[stage]][number, step - 1]
        return value

    row8 = iota((8, ATOMS), 0)
    lane8 = iota((8, ATOMS), 1)

    own_rows[...] = jnp.zeros((8, ATOMS), F32)
    for axis in range(3):
        own_rows[axis:axis + 1, :] = positions[axis, 0, 0]
    element = elements[0, 0]
    own_rows[3:4, :] = element.astype(F32)
    own_rows[4:5, :] = prior[0, 0]
    own = own_rows[...]

    ledger[0] = jnp.zeros((8, ATOMS), F32)
    ledger[0, 0:1, 0:32] = boundary[0, 0].astype(F32)
    picks = ledger[0]
    picks = picks + pltpu.roll(picks, 32, 1)
    picks = picks + pltpu.roll(picks, 64, 1)
    picks = jnp.broadcast_to(picks[0:1, :], (8, ATOMS)).astype(jnp.int32)
    places_in[...] = take_lanes(own, picks)

    pl.semaphore_wait(barrier, len(partners))
    send_blocks(places_in, places_got, 0)

    lengths = [DOMAIN * sizes[name] for name in AXES]

    def harmonics_of(places):
        for axis, name in enumerate(AXES):
            angle = (2.0 * math.pi / lengths[axis]) * (places[axis] + DOMAIN * at[name].astype(F32))
            c1, s1 = jnp.cos(angle), jnp.sin(angle)
            c, s = c1, s1
            for order in range(8):
                harmonics[2 * axis, order] = c
                harmonics[2 * axis + 1, order] = s
                c, s = c * c1 - s * s1, s * c1 + c * s1

    def first_factors(row):
        return jnp.concatenate([harmonics[0, :, row, :], harmonics[1, :, row, :]], axis=0)

    def phases_of(row):
        zc, zs = harmonics[4, :, row, :], harmonics[5, :, row, :]
        sums_c, sums_s, gaps_c, gaps_s = [], [], [], []
        for order in range(6):
            yc = jnp.broadcast_to(harmonics[2, order, row:row + 1, :], (8, ATOMS))
            ys = jnp.broadcast_to(harmonics[3, order, row:row + 1, :], (8, ATOMS))
            cc, ss, sc, cs = yc * zc, ys * zs, ys * zc, yc * zs
            sums_c.append(cc - ss)
            sums_s.append(sc + cs)
            gaps_c.append(cc + ss)
            gaps_s.append(sc - cs)
        rest = [jnp.zeros((ATOMS - WAVE_LANES, ATOMS), F32)]
        return jnp.concatenate(sums_c + gaps_c + rest + sums_s + gaps_s + rest, axis=0)

    harmonics_of([jnp.broadcast_to(own[axis:axis + 1, :], (8, ATOMS)) for axis in range(3)])
    own_first = first_factors(0)
    own_phases = phases_of(0)
    phases[...] = own_phases
    phases_t[...] = own_phases.T

    def structure(vector):
        return dot(own_first * vector, phases_t[...], HIGHEST)

    def packed(s):
        return jnp.concatenate([s[:, 0:ATOMS], s[:, ATOMS:]], axis=0)

    part = packed(structure(own[4:5, :]))
    send_part(0, 0, part)

    kx, ky, kz = waves[0:1, :], waves[1:2, :], waves[2:3, :]
    flip = jnp.where(kx > 0, 1, -1)
    ky, kz = ky * flip, kz * flip
    order = jnp.abs(kx) - 1
    spot = jnp.where(ky * kz > 0, 0, 48) + (jnp.abs(ky) - 1) * 8 + jnp.abs(kz) - 1
    waves_n = waves.shape[1]
    left = jnp.where(ky > 0, order, order + 8)
    left = (iota((16, waves_n), 0) == left).astype(F32).astype(BF16)
    right = (iota((ATOMS, waves_n), 0) == spot).astype(F32).astype(BF16)
    tally = lax.dot_general(left, right, (((1,), (1,)), ((), ())), preferred_element_type=F32)
    sign_lane = jnp.where(lane8 >= 48, lane8 - 48, lane8)
    mid_order = lax.shift_right_logical(sign_lane, 3) + 1
    last_order = jnp.bitwise_and(sign_lane, 7) + 1
    squared = jnp.zeros((8, ATOMS), F32)
    for axis, number in enumerate((row8 + 1, mid_order, last_order)):
        wave = (2.0 * math.pi / lengths[axis]) * number.astype(F32)
        squared = squared + wave * wave
    all_atoms = ATOMS * sizes["gx"] * sizes["gy"] * sizes["gz"]
    weight = COUPLING * DAMPING**2 * jnp.exp(-squared / (4.0 * DAMPING**2)) / (squared * all_atoms)
    even = weight * (tally[0:8] + tally[8:16])
    odd = weight * (tally[0:8] - tally[8:16])

    def weighted(s):
        cc, sc, cs, ss = s[0:8], s[8:16], s[16:24], s[24:32]
        return jnp.concatenate(
            [even * cc - odd * ss, even * sc + odd * cs, even * cs + odd * sc, even * ss - odd * cc], axis=0
        )

    ledger[0] = jnp.zeros((8, ATOMS), F32)
    for number, table in enumerate((chi_bias, short_bias, short_charge, chi_out, short_out)):
        for kind in range(ELEM):
            ledger[0, number:number + 1, kind * HID:(kind + 1) * HID] = table[kind:kind + 1, :]
    columns = jnp.concatenate([ledger[0], jnp.zeros((ATOMS - 8, ATOMS), F32)], axis=0).T

    owns = [(element == kind).astype(F32) for kind in range(ELEM)]
    stiffness = functools.reduce(lambda a, b: a + b, [hardness[kind] * owns[kind] for kind in range(ELEM)])
    unit_kind = lax.shift_right_logical(iota((ATOMS, ATOMS), 0), 5)
    unit_mask = (unit_kind == element).astype(F32)

    def network(inputs, weights, bias, mid, out_column, offset, extra=None):
        activation = dot(weights, inputs) + columns[:, bias:bias + 1]
        if extra is not None:
            activation = activation + extra
        first = (jnp.tanh(activation) * unit_mask).astype(BF16)
        second = jnp.tanh(dot(mid, first))
        chosen = jnp.zeros((HID, ATOMS), F32)
        for kind in range(ELEM):
            chosen = chosen + columns[kind * HID:(kind + 1) * HID, out_column:out_column + 1] * owns[kind]
        result = jnp.sum(second * chosen, axis=0, keepdims=True)
        for kind in range(ELEM):
            result = result + offset[kind] * owns[kind]
        return result

    listed = neighbours[0, 0, 0].astype(F32).T.astype(jnp.int32)
    lanes[...] = jnp.bitwise_and(listed, ATOMS - 1)
    chunks[...] = lax.shift_right_logical(listed, 7)

    block = 4 * (row8 - 1) + lax.shift_right_logical(lane8, 5)

    def extended(own_row, slots, row):
        value = jnp.where(row8 == 0, own_row, 0.0)
        for number in range(BLOCKS):
            value = jnp.where(block == number, slots[number, row:row + 1, :], value)
        return value

    def gathered(values):
        result = None
        which = chunks[...]
        where = lanes[...]
        for number in range(8):
            table = jnp.broadcast_to(values[number:number + 1, :], (ATOMS, ATOMS))
            picked = take_lanes(table, where)
            result = picked if result is None else jnp.where(which == number, picked, result)
        return result

    wait_blocks(places_got, halo_recv, 0)
    offset_index = jnp.where(block >= 13, block + 1, block)
    digit_x = jnp.where(offset_index >= 18, 1, jnp.where(offset_index >= 9, 0, -1))
    within = offset_index - 9 * (digit_x + 1)
    digit_y = jnp.where(within >= 6, 1, jnp.where(within >= 3, 0, -1))
    digit_z = within - 3 * (digit_y + 1) - 1
    ghost = (row8 > 0) & (block < BLOCKS)
    spaces = []
    for axis, digit in enumerate((digit_x, digit_y, digit_z)):
        spaces.append(extended(own[axis:axis + 1, :], places_got, axis) + jnp.where(ghost, DOMAIN * digit.astype(F32), 0.0))
    kinds = extended(own[3:4, :], places_got, 3)
    charge = extended(own[4:5, :], places_got, 4)

    apart = jnp.zeros((ATOMS, ATOMS), F32)
    for axis in range(3):
        gap = gathered(spaces[axis]) - own[axis:axis + 1, :]
        apart = apart + gap * gap
    distance = jnp.sqrt(apart)
    valid = (iota((ATOMS, ATOMS), 0) < counts[0, 0]).astype(F32)
    soft = jnp.sqrt(apart + SOFTENING * SOFTENING)
    pair[...] = valid * (PAIR_STRENGTH / ATOMS) * SOFTENING * (1.0 - lax.erf(SCREENING * soft)) / soft
    falloff[...] = valid * 0.5 * (1.0 + jnp.cos(math.pi * jnp.minimum(distance, CUTOFF) / CUTOFF))
    spans[...] = distance
    near_kinds = gathered(kinds)
    for kind in range(ELEM):
        seen[kind] = (near_kinds == float(kind)).astype(F32)

    part = summed(0, 0, part)
    send_part(0, 1, part)

    def local_part(values):
        return stiffness * values[0:1, :] + jnp.sum(pair[...] * gathered(values), axis=0, keepdims=True)

    spacing = CUTOFF / (NBASIS - 1)

    def descriptors(base):
        def step(number, carry):
            centre = spacing * lax.convert_element_type(number, F32)
            scaled = (spans[...] - centre) / spacing
            basis = jnp.exp(-0.5 * (scaled * scaled)) * falloff[...]
            for kind in range(ELEM):
                tables[pl.ds(base + kind * NBASIS + number, 1), :] = jnp.sum(basis * seen[kind], axis=0, keepdims=True)
            return carry
        lax.fori_loop(0, NBASIS, step, 0)

    start_local = local_part(charge)
    descriptors(0)
    part = summed(0, 1, part)
    send_part(0, 2, part)
    features = (FEATURE_SCALE * tables[0:ATOMS, :]).astype(BF16)
    negativity = network(features, chi_first[...], 0, chi_mid[...], 3, chi_offset)

    def send_row(row, index):
        row_out[index] = take_lanes(jnp.broadcast_to(row, (8, ATOMS)), picks)[0:1, :]
        send_blocks(row_out.at[index], row_got.at[index], index + 1)

    def extended_row(row, index):
        wait_blocks(row_got.at[index], halo_recv, index + 1)
        return extended(row, row_got.at[index], 0)

    known = negativity + start_local
    send_row(known, 0)

    harmonics_of(spaces)
    ghost_first = []
    for row in range(1, 8):
        ghost_first.append(first_factors(row))
        coarse[:, (row - 1) * ATOMS:row * ATOMS] = phases_of(row).astype(BF16)

    def spread(u):
        u = jnp.concatenate([u[0:16], u[16:32]], axis=1)
        mine = jnp.sum(own_first * dot(u, phases[...], HIGHEST), axis=0, keepdims=True)
        value = jnp.where(row8 == 0, mine, 0.0)
        theirs = dot(u.astype(BF16), coarse[...])
        for row in range(1, 8):
            piece = jnp.sum(ghost_first[row - 1] * theirs[:, (row - 1) * ATOMS:row * ATOMS], axis=0, keepdims=True)
            value = jnp.where(row8 == row, piece, value)
        return jnp.where((row8 == 0) | ghost, value, 0.0)

    part = summed(0, 2, part)
    potential = spread(weighted(part))
    residual = -(extended_row(known, 0) + potential)

    direction = image = local_direction = shape_direction = curvature = norm = None
    for step in range(ITERS):
        mine = residual[0:1, :]
        local = local_part(residual)
        rows = [mine * mine, mine * local]
        if step:
            rows += [mine * local_direction, direction[0:1, :] * local]
        products = jnp.concatenate(rows + [jnp.zeros((8 - len(rows), ATOMS), F32)], axis=0)
        products = jnp.sum(products, axis=1, keepdims=True)
        part = packed(structure(mine))
        top = jnp.where(lane8 == WAVE_LANES, products, part[0:8])
        part = jnp.concatenate([top, part[8:32]], axis=0)
        send_part(step + 1, 0, part)
        if step + 1 < ITERS:
            send_row(local, step + 1)
        part = summed(step + 1, 0, part)
        send_part(step + 1, 1, part)
        part = summed(step + 1, 1, part)
        send_part(step + 1, 2, part)
        part = summed(step + 1, 2, part)
        sums = [part[number:number + 1, WAVE_LANES:WAVE_LANES + 1] for number in range(4)]
        u = weighted(part)
        energy = part * u
        energy = total(energy[0:8] + energy[8:16] + energy[16:24] + energy[24:32])
        own_curvature = sums[1] + energy
        if step == 0:
            curvature = own_curvature
            direction, local_direction, shape_direction = residual, local, part
        else:
            ratio = sums[0] / norm
            cross = shape_direction * u
            cross = 2.0 * total(cross[0:8] + cross[8:16] + cross[16:24] + cross[24:32]) + sums[2] + sums[3]
            curvature = own_curvature + ratio * cross + ratio * ratio * curvature
            direction = residual + ratio * direction
            local_direction = local + ratio * local_direction
            shape_direction = part + ratio * shape_direction
        norm = sums[0]
        alpha = norm / curvature
        charge = charge + alpha * direction
        if step + 1 < ITERS:
            fresh = extended_row(local, step + 1) + spread(u)
            image = fresh if step == 0 else fresh + ratio * image
            residual = residual - alpha * image

    charges_out[0, 0] = charge[0:1, :]
    near_charge = gathered(charge)
    for kind in range(ELEM):
        seen[kind] = seen[kind] * near_charge
    descriptors(ATOMS)
    inputs = (FEATURE_SCALE * tables[...]).astype(BF16)
    energies_out[0, 0] = network(
        inputs, short_first[...], 1, short_mid[...], 4, short_offset,
        columns[:, 2:3] * charge[0:1, :],
    )

    wait_blocks(places_got, halo_send, 0)
    for index in range(ITERS):
        wait_blocks(row_got.at[index], halo_send, index + 1)
    for number in range(ITERS + 1):
        for stage, name in enumerate(STAGES):
            slots = got[name].at[number]
            pltpu.make_async_copy(slots, slots, sum_send.at[number, stage]).wait()


def solution(mesh):
    sizes = {name: mesh.shape[name] for name in AXES}

    def body(
        positions, elements, prior_charges, neighbours, counts, boundary, wave_numbers, hardness,
        chi_first, chi_bias, chi_mid, chi_out, chi_offset,
        short_first, short_charge, short_bias, short_mid, short_out, short_offset,
    ):
        vmem, smem = pl.BlockSpec(memory_space=pltpu.VMEM), pl.BlockSpec(memory_space=pltpu.SMEM)
        sums = ITERS + 1
        return pl.pallas_call(
            functools.partial(kernel, sizes),
            out_shape=[jax.ShapeDtypeStruct((1, 1, 1, ATOMS), F32)] * 2,
            in_specs=[vmem] * 7 + [smem] + [vmem] * 4 + [smem] + [vmem] * 5 + [smem],
            out_specs=[vmem] * 2,
            scratch_shapes=[
                pltpu.VMEM((8, ATOMS), F32),
                pltpu.VMEM((8, ATOMS), F32),
                pltpu.VMEM((BLOCKS, 8, ATOMS), F32),
                pltpu.VMEM((ITERS, 1, ATOMS), F32),
                pltpu.VMEM((ITERS, BLOCKS, 1, ATOMS), F32),
                pltpu.VMEM((sums, 3, 32, ATOMS), F32),
                pltpu.VMEM((sums, sizes["gy"] - 1, 32, ATOMS), F32),
                pltpu.VMEM((sums, sizes["gx"] - 1, 32, ATOMS), F32),
                pltpu.VMEM((sums, sizes["gz"] - 1, 32, ATOMS), F32),
                pltpu.VMEM((ATOMS, ATOMS), jnp.int32),
                pltpu.VMEM((ATOMS, ATOMS), jnp.int32),
                pltpu.VMEM((ELEM, ATOMS, ATOMS), F32),
                pltpu.VMEM((ATOMS, ATOMS), F32),
                pltpu.VMEM((ATOMS, ATOMS), F32),
                pltpu.VMEM((ATOMS, ATOMS), F32),
                pltpu.VMEM((2 * ATOMS, ATOMS), F32),
                pltpu.VMEM((6, 8, 8, ATOMS), F32),
                pltpu.VMEM((2 * ATOMS, ATOMS), F32),
                pltpu.VMEM((ATOMS, 2 * ATOMS), F32),
                pltpu.VMEM((2 * ATOMS, 7 * ATOMS), BF16),
                pltpu.VMEM((1, 8, ATOMS), F32),
                pltpu.SemaphoreType.DMA((ITERS + 1,)),
                pltpu.SemaphoreType.DMA((ITERS + 1,)),
                pltpu.SemaphoreType.DMA((sums, 3)),
                pltpu.SemaphoreType.DMA((sums, 3)),
            ],
            compiler_params=pltpu.CompilerParams(collective_id=0, has_side_effects=True),
        )(
            positions, elements, prior_charges, neighbours, counts, boundary.reshape(1, 1, 1, -1), wave_numbers,
            hardness, chi_first.reshape(ELEM * HID, -1), chi_bias, chi_mid.reshape(HID, -1), chi_out, chi_offset,
            short_first.reshape(ELEM * HID, -1), short_charge, short_bias, short_mid.reshape(HID, -1), short_out,
            short_offset,
        )

    cell = P("gx", "gy", "gz", None)
    return jax.shard_map(
        body,
        mesh=mesh,
        in_specs=(P(None, *cell), cell, cell, P(*cell, None), cell, cell) + (P(),) * 13,
        out_specs=(cell, cell),
        check_vma=False,
    )
```

time: 763 us -> 76.8 us (0.10)
  local copies, waits for them, and re-layouts: 401 us -> 3.92 us
  blocking collectives: 247 us -> 0 us
  Pallas kernels: 0 us -> 71.6 us
  starting transfers between devices: 52.1 us -> 0 us
  other arithmetic: 32.2 us -> 0 us
  between operations: 13.3 us -> 0.66 us
  waiting for transfers between devices: 10.5 us -> 0 us
    gather x11 -> x0, local copies, waits for them, and re-layouts: 389 us -> none  [the longest x4 261 us: local_apply(): return stiffness * vector + jnp.sum(kernel * values[neighbour_list], axis=1)]
    psum x16 -> x0, blocking collectives: 247 us -> none  [over_axes(): return functools.reduce(lax.psum, axes, x)]
    pallas_call x0 -> x1, Pallas kernels: none -> 71.6 us  [body(): pl.pallas_call(functools.partial(kernel, sizes), out_shape=[jax.ShapeDtyp...]
    ppermute x24 -> x0, starting transfers between devices: 52.1 us -> none  [the longest x12 26.5 us: with_halo(): before = lax.ppermute(last, axis, up)]
    reduce_sum x22 -> x0, other arithmetic: 20 us -> none  [the longest x2 6.09 us: contract_slots(): jnp.sum(basis * weights[kind][None], axis=2)]
    ppermute x24 -> x0, waiting for transfers between devices: 10.5 us -> none  [the longest x12 5.28 us: with_halo(): after = lax.ppermute(initial, axis, down)]
  transfers between devices with their start and end apart: 24 -> 0, of which waited for: 11 -> 0; matrix products, arithmetic and copies ran while one was open for 2% -> 0% of each run, Pallas kernels for 0% -> 0%
where the time goes in v1:
time: 76.8 us; the launch traced here: 76.2 us
  Pallas kernels  71.6 us (93%)
  local copies, waits for them, and re-layouts  3.92 us (5%)
    pallas_call x1, Pallas kernels, body(): pl.pallas_call(functools.partial(kernel, sizes), out_shape=[jax.ShapeDtyp...  71.6 us
    unnamed x8, local copies, waits for them, and re-layouts  1.78 us

profile of v1, /device:TPU:1, one launch (start us, length us, event | category | flops | bytes accessed | tf_op | source)
XLA Modules:
  0.0 76.2 jit_solution(6196065284144078453)
XLA Ops:
  0.6 0.0 copy-start
  0.6 1.4 %reshape.17.chi_mid = bf16[32,128]{1,0:T(8,128)(2,1)} reshape(bf16[32,4,32]{2,1,0:T(4,128)(2,1)} %param.29) | data formatting | bytes 16384 | tf_op jit(solution)/shard_map/reshape | solution.py:444
  2.1 0.0 copy-done
  2.1 0.7 reshape.19.short_mid
  2.8 71.6 %shard_map.194 = (f32[1,1,1,128]{3,2,1,0:T(1,128)}, f32[1,1,1,128]{3,2,1,0:T(1,128)}) custom-call(f32[3,1,1,1,128]{4,3,2,1,0:T(1,128)} %positions.1, s32[1,1,1,128]{3,2,1,0:T(1,128)} %elements.1, f32[1,1,1,128]{3,2,1,0:T(1,128)} %prior.1, s32[1,1,1,128,128]{4,3,2,1,0:T(8,128)} %neighbours.1, s32[1,1,1,128]{3,2,1,0:T(1,128)} %counts.1, ...), custom_call_target="tpu_custom_call" | custom-call | tf_op jit(solution)/shard_map/pallas_call | solution.py:409
  74.4 0.0 copy-start.2
  74.4 0.6 copy-done.2
  75.0 0.0 copy-start.1
  75.0 0.5 copy.23
  75.5 0.2 copy-done.1
  75.7 0.5 copy.24
Async XLA Ops:
  0.6 1.5 %copy-start = (bf16[32,4,32]{2,1,0:T(4,128)(2,1)S(1)}, bf16[32,4,32]{2,1,0:T(4,128)(2,1)}, u32[]{:S(2)}) copy-start(bf16[32,4,32]{2,1,0:T(4,128)(2,1)} %param.35) | copy-start | bytes 24580
  74.4 0.6 copy-start.2
  75.0 0.7 copy-start.1
